TPU v7x, 32 devices: a whole 2x2x4 slice. The times are simulated.
32 devices in a mesh: blk: 16 (over z, x, core), cuts: 2 (over y).
Axes of the slice: x: 2, y: 2, z: 4, core: 2. Of those that a mesh axis runs over, the one named last changes fastest.
Arguments:
- left_env: bfloat16 [2048, 8, 2048], P('blk', 'cuts'), may hold values from -4 to 4
- right_env: bfloat16 [2048, 8, 2048], P('blk', 'cuts'), may hold values from -4 to 4
- left_core: float32 [8, 8, 2, 2], replicated, may hold values from -1.5 to 1.5
- right_core: float32 [8, 8, 2, 2], replicated, may hold values from -1.5 to 1.5
- slot_bond: int32 [8], replicated, may hold values from 0 to 7, each once
- krylov_basis: float32 [8, 2048, 4, 2048], P(None, 'blk', None, 'cuts'), may hold values from -30 to 30
- beta_prev: float32 [], replicated, may hold values from 0.3 to 1.2
Outputs:
- next_vector: float32 [2048, 4, 2048], P('blk', None, 'cuts')
- alpha_values: float32 [1], replicated
- beta_values: float32 [1], replicated
Inputs may be any that keep to these rules, and one draw needn't show every extreme that they name: `slot_bond`: a permutation of the 8 bond values.
All inputs are finite; a program needn't handle non-finite values.
Results may differ from a plain program's by a relative error of at most 0.00073.
The roundings to bfloat16 on the way count: a program that leaves them out, or rounds other values in their place, can miss the bound.
Values may be sent and summed in bfloat16 or wider, within the bound.
A program may use at most 192 MiB of HBM per device.

v0:
```python
import jax
import jax.numpy as jnp
from jax import lax
from jax.sharding import PartitionSpec as P


def build_table(left_core, right_core, slot_bond):
    bond_width = left_core.shape[0]
    phys_dim = left_core.shape[2]
    chosen = (slot_bond[:, None] == jnp.arange(bond_width, dtype=jnp.int32)[None, :]).astype(
        jnp.float32
    )
    picked = jnp.einsum("kw,wxac->kxac", chosen, left_core, precision=lax.Precision.HIGHEST)
    table = jnp.einsum("kxac,xybd->kyabcd", picked, right_core, precision=lax.Precision.HIGHEST)
    return table.reshape(bond_width, bond_width, phys_dim * phys_dim, phys_dim * phys_dim)


def on_device(left_env, right_env, left_core, right_core, slot_bond, krylov_basis, beta_prev):
    highest = lax.Precision.HIGHEST
    bond_width = left_core.shape[0]
    pair_count = left_core.shape[2] * left_core.shape[2]
    basis_count = krylov_basis.shape[0]
    row_count = krylov_basis.shape[1]
    col_count = krylov_basis.shape[3]
    full_width = left_env.shape[2]
    entries = float(full_width * pair_count * full_width)
    mpo_table = build_table(left_core, right_core, slot_bond)
    left_full = lax.all_gather(left_env, "cuts", axis=1, tiled=True)
    left_matrix = left_full.reshape(row_count * bond_width, full_width)
    right_local = lax.all_to_all(right_env, "cuts", split_axis=2, concat_axis=1, tiled=True)
    next_vector = krylov_basis[basis_count - 1]
    current_f = krylov_basis[basis_count - 1]
    previous = krylov_basis[basis_count - 2]
    current = current_f.astype(jnp.bfloat16)
    block_rows = lax.all_gather(current, "blk", axis=0, tiled=True)
    count_rows = block_rows.shape[0]
    projected = jnp.dot(
        left_matrix,
        block_rows.reshape(count_rows, pair_count * col_count),
        preferred_element_type=jnp.float32,
    )
    projected = projected.reshape(row_count, bond_width, pair_count, col_count)
    mixed_left = jnp.einsum("kypq,akqb->apyb", mpo_table, projected, precision=highest).astype(
        jnp.bfloat16
    )
    left_side = mixed_left.reshape(row_count * pair_count, bond_width * col_count)
    block_rows = lax.all_gather(right_local, "blk", axis=0, tiled=True)
    flat_rows = block_rows.reshape(block_rows.shape[0], -1)
    partial_terms = lax.dot_general(
        left_side, flat_rows, (((1,), (1,)), ((), ())), preferred_element_type=jnp.float32
    )
    image_vec = lax.psum_scatter(
        partial_terms.reshape(row_count, pair_count, full_width),
        "cuts",
        scatter_dimension=2,
        tiled=True,
    )
    local_gram = jnp.einsum("japb,kapb->jk", krylov_basis, krylov_basis, precision=highest)
    gram_matrix = lax.psum(local_gram, ("blk", "cuts")) / entries
    local_prods = jnp.einsum("japb,apb->j", krylov_basis, image_vec, precision=highest)
    inner_prods, image_square = lax.psum(
        (local_prods, jnp.sum(image_vec * image_vec)), ("blk", "cuts")
    )
    inner_prods = inner_prods / entries
    image_square = image_square / entries
    alpha_now = inner_prods[basis_count - 1]
    ortho_coeffs = (
        inner_prods
        - alpha_now * gram_matrix[:, basis_count - 1]
        - beta_prev * gram_matrix[:, basis_count - 2]
    )
    first_square = (
        image_square
        - 2.0 * alpha_now * inner_prods[basis_count - 1]
        - 2.0 * beta_prev * inner_prods[basis_count - 2]
        + alpha_now * alpha_now * gram_matrix[basis_count - 1, basis_count - 1]
        + 2.0 * alpha_now * beta_prev * gram_matrix[basis_count - 1, basis_count - 2]
        + beta_prev * beta_prev * gram_matrix[basis_count - 2, basis_count - 2]
    )
    square_mean = (
        first_square
        - 2.0 * jnp.sum(ortho_coeffs * ortho_coeffs)
        + jnp.sum(ortho_coeffs[:, None] * gram_matrix * ortho_coeffs[None, :])
    )
    first_pass = image_vec - alpha_now * current_f - beta_prev * previous
    second_pass = first_pass - jnp.einsum(
        "j,japb->apb", ortho_coeffs, krylov_basis, precision=highest
    )
    beta_new = jnp.sqrt(square_mean + 1e-06)
    next_vector = second_pass / beta_new
    alpha_list = [alpha_now]
    beta_list = [beta_new]
    return (next_vector, jnp.stack(alpha_list), jnp.stack(beta_list))


def solution(mesh):
    in_specs = (
        P("blk", "cuts", None),
        P("blk", "cuts", None),
        P(),
        P(),
        P(),
        P(None, "blk", None, "cuts"),
        P(),
    )
    out_specs = (P("blk", None, "cuts"), P(), P())
    return jax.shard_map(
        on_device, mesh=mesh, in_specs=in_specs, out_specs=out_specs, check_vma=False
    )
```

profile of v0, /device:TPU:0, one launch (start us, length us, event | category | flops | bytes accessed | tf_op | source)
XLA Modules:
  0.0 616.2 jit_solution(4557364010513093199)
XLA Ops:
  7.2 4.5 fusion.43
  11.7 1.3 copy-done.3
  13.1 2.1 copy.113
  15.2 0.0 all-gather.5.cloned.1.call-start
  15.2 2.5 copy.42
  17.8 0.0 all-gather.7.cloned.1.call-start
  17.8 5.6 copy.50
  23.4 30.2 %all_to_all.18 = bf16[128,4,2048]{0,1,2:T(4,128)(2,1)S(1)} all-to-all(bf16[128,4,2048]{0,1,2:T(4,128)(2,1)} %copy.50), channel_id=1, replica_groups=mesh['blk'=16,'cuts'=2] {'cuts'}, dimensions={2} | all-to-all | bytes 4194304 | tf_op jit(solution)/shard_map/all_to_all | solution.py:30
  53.6 2.7 copy.51
  56.3 0.0 reduce-scatter.2.cloned.1.call-start
  56.4 0.2 convolution_bitcast_fusion.1
  56.5 0.2 convolution_bitcast_fusion
  56.7 0.6 copy.48
  57.4 87.1 %all-gather.9.cloned.1.call-done = bf16[1,2048,4,1024]{3,1,2,0:T(8,128)(2,1)} async-done(((bf16[1,128,4,1024]{3,1,2,0:T(8,128)(2,1)}), bf16[1,2048,4,1024]{3,1,2,0:T(8,128)(2,1)}) %all-gather.9.cloned.1.call-update) | async-done | bytes 16777232 | tf_op jit(solution)/shard_map/all_gather | solution.py:35
  144.5 22.2 %copy.44 = bf16[1,2048,4,1024]{1,3,2,0:T(8,128)(2,1)} copy(bf16[1,2048,4,1024]{3,1,2,0:T(8,128)(2,1)} %all-gather.9.cloned.1.call-done) | data formatting | bytes 33554432 | tf_op jit(solution)/shard_map/all_gather | solution.py:35
  166.7 34.2 %all-gather.5.cloned.1.call-done = bf16[128,8,2048]{2,0,1:T(8,128)(2,1)} async-done(((bf16[128,4,2048]{2,0,1:T(8,128)(2,1)}), bf16[128,8,2048]{2,0,1:T(8,128)(2,1)}) %all-gather.5.cloned.1.call-update) | async-done | bytes 4194320 | tf_op jit(solution)/shard_map/all_gather | solution.py:28
  201.0 25.6 %fusion.4 = f32[128,8,4,1024]{3,1,2,0:T(8,128)} fusion(bf16[1,2048,4,1024]{1,3,2,0:T(8,128)(2,1)} %copy.44, bf16[128,8,2048,1]{2,0,1,3:T(8,128)(2,1)} %bitcast.94), kind=kOutput, calls=%fused_computation.4 | convolution fusion | flops 17179869184 | bytes 37748736 | tf_op jit(solution)/shard_map/dot_general | solution.py:37
  226.6 20.6 %fusion.15 = bf16[128,4,8,1024]{3,2,1,0:T(8,128)(2,1)} fusion(f32[8,8,4,4,1]{1,0,3,2,4:T(8,128)S(1)} %bitcast.93, f32[128,8,4,1024]{3,1,2,0:T(8,128)} %fusion.4), kind=kOutput, calls=%fused_computation.14 | convolution fusion | flops 1614807040 | bytes 25169920 | tf_op jit(solution)/shard_map/kypq,akqb->apyb/dot_general | solution.py:43
  247.2 123.4 %all-gather.7.cloned.1.call-done = bf16[2048,8,1024]{2,0,1:T(8,128)(2,1)} async-done(((bf16[128,8,1024]{2,0,1:T(8,128)(2,1)}), bf16[2048,8,1024]{2,0,1:T(8,128)(2,1)}) %all-gather.7.cloned.1.call-update) | async-done | bytes 33554448 | tf_op jit(solution)/shard_map/all_gather | solution.py:47
  370.6 46.7 %fusion.19 = f32[128,4,2048]{2,0,1:T(8,128)} fusion(bf16[2048,8,1024]{2,0,1:T(8,128)(2,1)} %all-gather.7.cloned.1.call-done, bf16[128,4,8,1024]{3,2,1,0:T(8,128)(2,1)} %fusion.15), kind=kOutput, calls=%fused_computation.16 | convolution fusion | flops 17179869184 | bytes 46137344 | tf_op jit(solution)/shard_map/dot_general | solution.py:49
  418.0 54.5 %fusion.29 = f32[8,8]{1,0:T(8,128)S(1)} fusion(f32[8,128,4,1024]{3,2,1,0:T(4,128)} %param.12), kind=kOutput, calls=%fused_computation.28 | convolution fusion | flops 402653184 | bytes 16777472 | tf_op jit(solution)/shard_map/japb,kapb->jk/dot_general | solution.py:58
  472.5 43.3 %fusion.32 = f32[8]{0:T(128)S(1)} fusion(f32[8,128,4,1024]{3,2,1,0:T(4,128)} %param.12, f32[128,4,1024,1]{2,0,1,3:T(8,128)} %bitcast.90), kind=kOutput, calls=%fused_computation.29 | convolution fusion | flops 50331648 | bytes 18874400 | tf_op jit(solution)/shard_map/japb,apb->j/dot_general | solution.py:60
  515.8 1.1 multiply_reduce_fusion
  517.0 39.9 %all-reduce = (f32[8,8]{1,0:T(8,128)S(1)}, f32[8]{0:T(128)S(1)}, f32[]{:T(128)}) all-reduce(f32[8,8]{1,0:T(8,128)S(1)} %fusion.29, f32[8]{0:T(128)S(1)} %fusion.32, f32[]{:T(128)} %multiply_reduce_fusion), channel_id=1, replica_groups=mesh['blk'=16,'cuts'=2] {'blk','cuts'}, use_global_device_ids=true, to_apply=%region_2.0 | all-reduce | flops 73 | bytes 584 | tf_op jit(solution)/shard_map/psum | solution.py:59
  556.9 0.6 fusion.45
  559.5 0.9 multiply_reduce_fusion.3
  560.3 0.7 fusion.44
  561.7 0.7 multiply_reduce_fusion.4
  562.3 30.8 %fusion.6 = f32[1,128,4,1024]{3,0,2,1:T(1,128)} fusion(f32[8,128,4,1024]{3,2,1,0:T(4,128)} %param.12, f32[8]{0:T(128)S(1)} %get-tuple-element.21), kind=kOutput, calls=%fused_computation.7 | convolution fusion | flops 50331648 | bytes 18874400 | tf_op jit(solution)/shard_map/j,japb->apb/dot_general | solution.py:86
  593.1 0.7 multiply_reduce_fusion.1
  598.4 6.9 %fusion.27 = f32[128,4,1024]{2,0,1:T(8,128)S(1)} fusion(f32[1,128,4,1024]{3,2,1,0:T(4,128)} %get-tuple-element.23, f32[128,4,1024]{2,0,1:T(8,128)S(1)} %copy-done.2, f32[1,128,4,1024]{3,0,2,1:T(1,128)} %fusion.6, f32[1,128,4,1024]{3,2,1,0:T(4,128)} %copy-done.3, f32[]{:T(128)} %sqrt.3, f32[]{:T(128)S(6)} %copy.114, f32[]{:T(128)} %bitcast.27), kind=kLoop, calls=%fused_computation.21 | loop fusion | flops 3145728 | bytes 10485772 | tf_op jit(solution)/shard_map/div | solution.py:90
  605.3 2.7 copy.56
  (24 shorter events, 0.2 us)
Async XLA Ops:
  7.2 49.4 %copy-start = (f32[8,8,2,2]{1,3,2,0:T(2,128)S(1)}, f32[8,8,2,2]{1,3,2,0:T(2,128)}, u32[]{:S(2)}) copy-start(f32[8,8,2,2]{1,3,2,0:T(2,128)} %param.10) | copy-start | bytes 3076
  7.2 137.3 %all-gather.9.cloned.1.call-start = ((), (), s32[]{:S(2)}) async-start(), calls=%async_computation.5 | async-start | bytes 17825792 | tf_op jit(solution)/shard_map/all_gather | solution.py:35
  11.7 1.3 copy-start.3
  11.7 3.5 copy-start.4
  15.2 185.8 %all-gather.5.cloned.1.call-start = ((), (), s32[]{:S(2)}) async-start(), calls=%async_computation.2 | async-start | bytes 6291456 | tf_op jit(solution)/shard_map/all_gather | solution.py:28
  17.8 352.9 %all-gather.7.cloned.1.call-start = ((), (), s32[]{:S(2)}) async-start(), calls=%async_computation.3 | async-start | bytes 35651584 | tf_op jit(solution)/shard_map/all_gather | solution.py:47
  53.6 2.8 copy-start.6
  53.6 2.8 copy-start.7
  56.3 416.2 %reduce-scatter.2.cloned.1.call-start = ((), (), s32[]{:S(2)}) async-start(), calls=%async_computation.4 | async-start | bytes 6291456 | tf_op jit(solution)/shard_map/reduce_scatter | solution.py:52
  201.0 25.6 %copy-start.5 = (f32[8,8,2,2,2,2]{1,0,5,4,3,2:T(8,128)S(1)}, f32[8,8,2,2,2,2]{1,0,5,4,3,2:T(8,128)}, u32[]{:S(2)}) copy-start(f32[8,8,2,2,2,2]{1,0,5,4,3,2:T(8,128)} %copy.48) | copy-start | bytes 12292
  472.5 43.3 %copy-start.2 = (f32[128,4,1024]{2,0,1:T(8,128)S(1)}, f32[128,4,1024]{2,0,1:T(8,128)}, u32[]{:S(2)}) copy-start(f32[128,4,1024]{2,0,1:T(8,128)} %reduce-scatter.2.cloned.1.call-done) | copy-start | bytes 6291460
  598.4 9.6 %copy-start.1 = (f32[8,8,2,2]{1,3,2,0:T(2,128)S(1)}, f32[8,8,2,2]{1,3,2,0:T(2,128)}, u32[]{:S(2)}) copy-start(f32[8,8,2,2]{1,3,2,0:T(2,128)} %param.10) | copy-start | bytes 3076
Sparse Core Ops, SparseCore 0:
  15.3 129.1 all-gather.8
  146.0 54.8 all-gather.4
  202.5 168.0 all-gather.6
  417.5 54.3 reduce-scatter.1
where the time goes:
time: 624 us; the launch traced here: 616 us
  waiting for transfers between devices  245 us (39%)
  matrix products  222 us (36%)
  blocking collectives  70.1 us (11%)
  local copies, waits for them, and re-layouts  45.5 us (7%)
  between operations  23.3 us (4%)
  other arithmetic  10.3 us (2%)
    all_gather x1, waiting for transfers between devices, on_device(): block_rows = lax.all_gather(right_local, 'blk', axis=0, tiled=True)  123 us
    all_gather x1, waiting for transfers between devices, on_device(): block_rows = lax.all_gather(current, 'blk', axis=0, tiled=True)  87.1 us
    dot_general x1, matrix products, on_device(): jnp.einsum('japb,kapb->jk', krylov_basis, krylov_basis, precision=highest)  54.5 us
    dot_general x1, matrix products, on_device(): lax.dot_general(left_side, flat_rows, (((1,), (1,)), ((), ())), preferred...  46.7 us
    dot_general x1, matrix products, on_device(): jnp.einsum('japb,apb->j', krylov_basis, image_vec, precision=highest)  43.3 us
    psum x1, blocking collectives, on_device(): gram_matrix = lax.psum(local_gram, ('blk', 'cuts')) / entries  39.9 us
    all_gather x1, waiting for transfers between devices, on_device(): left_full = lax.all_gather(left_env, 'cuts', axis=1, tiled=True)  34.2 us
    dot_general x1, matrix products, on_device(): jnp.einsum('j,japb->apb', ortho_coeffs, krylov_basis, precision=highest)  30.8 us
  transfers between devices with their start and end apart: 4, of which 3 were waited for; matrix products, arithmetic and copies ran while one was open for 22% of the time, Pallas kernels for 0%

commit v1 on v0

--- a/solution.py
+++ b/solution.py
@@ -56,7 +56,7 @@
         tiled=True,
     )
     local_gram = jnp.einsum("japb,kapb->jk", krylov_basis, krylov_basis, precision=highest)
-    gram_matrix = lax.psum(local_gram, ("blk", "cuts")) / entries
+    gram_matrix = jnp.sum(lax.all_gather(local_gram, ("blk", "cuts")), axis=0) / entries
     local_prods = jnp.einsum("japb,apb->j", krylov_basis, image_vec, precision=highest)
     inner_prods, image_square = lax.psum(
         (local_prods, jnp.sum(image_vec * image_vec)), ("blk", "cuts")

time: 624 us -> 689 us (1.10)
  blocking collectives: 70.1 us -> 135 us
    all_gather x0 -> x1, blocking collectives: none -> 68 us  [on_device(): lax.all_gather(local_gram, ('blk', 'cuts'))]
  transfers between devices with their start and end apart: 4 -> 4, of which waited for: 3 -> 3; matrix products, arithmetic and copies ran while one was open for 22% -> 20% of each run, Pallas kernels for 0% -> 0%
where the time goes in v1:
time: 689 us; the launch traced here: 681 us
  waiting for transfers between devices  245 us (36%)
  matrix products  222 us (32%)
  blocking collectives  135 us (20%)
  local copies, waits for them, and re-layouts  45.5 us (7%)
  between operations  22.8 us (3%)
  other arithmetic  10.3 us (1%)
    all_gather x1, waiting for transfers between devices, on_device(): block_rows = lax.all_gather(right_local, 'blk', axis=0, tiled=True)  123 us
    all_gather x1, waiting for transfers between devices, on_device(): block_rows = lax.all_gather(current, 'blk', axis=0, tiled=True)  87.1 us
    all_gather x1, blocking collectives, on_device(): lax.all_gather(local_gram, ('blk', 'cuts'))  68 us
    dot_general x1, matrix products, on_device(): jnp.einsum('japb,kapb->jk', krylov_basis, krylov_basis, precision=highest)  54.5 us
    dot_general x1, matrix products, on_device(): lax.dot_general(left_side, flat_rows, (((1,), (1,)), ((), ())), preferred...  46.6 us
    dot_general x1, matrix products, on_device(): jnp.einsum('japb,apb->j', krylov_basis, image_vec, precision=highest)  43.3 us
    psum x1, blocking collectives, on_device(): lax.psum((local_prods, jnp.sum(image_vec * image_vec)), ('blk', 'cuts'))  37.1 us
    all_gather x1, waiting for transfers between devices, on_device(): left_full = lax.all_gather(left_env, 'cuts', axis=1, tiled=True)  34.2 us
  transfers between devices with their start and end apart: 4, of which 3 were waited for; matrix products, arithmetic and copies ran while one was open for 20% of the time, Pallas kernels for 0%

profile of v1, /device:TPU:0, one launch (start us, length us, event | category | flops | bytes accessed | tf_op | source)
XLA Modules:
  0.0 680.9 jit_solution(4909270385145004269)
XLA Ops:
  7.2 4.5 fusion.43
  11.7 1.3 copy-done.3
  13.1 2.1 copy.128
  15.2 0.0 all-gather.6.cloned.1.call-start
  15.2 2.5 copy.57
  17.8 0.0 all-gather.8.cloned.1.call-start
  17.8 5.6 copy.65
  23.4 30.2 %all_to_all.18 = bf16[128,4,2048]{0,1,2:T(4,128)(2,1)S(1)} all-to-all(bf16[128,4,2048]{0,1,2:T(4,128)(2,1)} %copy.65), channel_id=1, replica_groups=mesh['blk'=16,'cuts'=2] {'cuts'}, dimensions={2} | all-to-all | bytes 4194304 | tf_op jit(solution)/shard_map/all_to_all | solution.py:30
  53.6 2.7 copy.66
  56.4 0.2 convolution_bitcast_fusion.1
  56.6 0.2 convolution_bitcast_fusion
  56.8 0.6 copy.63
  57.4 87.1 %all-gather.10.cloned.1.call-done = bf16[1,2048,4,1024]{3,1,2,0:T(8,128)(2,1)} async-done(((bf16[1,128,4,1024]{3,1,2,0:T(8,128)(2,1)}), bf16[1,2048,4,1024]{3,1,2,0:T(8,128)(2,1)}) %all-gather.10.cloned.1.call-update) | async-done | bytes 16777232 | tf_op jit(solution)/shard_map/all_gather | solution.py:35
  144.5 22.3 %copy.59 = bf16[1,2048,4,1024]{1,3,2,0:T(8,128)(2,1)} copy(bf16[1,2048,4,1024]{3,1,2,0:T(8,128)(2,1)} %all-gather.10.cloned.1.call-done) | data formatting | bytes 33554432 | tf_op jit(solution)/shard_map/all_gather | solution.py:35
  166.8 34.2 %all-gather.6.cloned.1.call-done = bf16[128,8,2048]{2,0,1:T(8,128)(2,1)} async-done(((bf16[128,4,2048]{2,0,1:T(8,128)(2,1)}), bf16[128,8,2048]{2,0,1:T(8,128)(2,1)}) %all-gather.6.cloned.1.call-update) | async-done | bytes 4194320 | tf_op jit(solution)/shard_map/all_gather | solution.py:28
  201.0 25.6 %fusion.4 = f32[128,8,4,1024]{3,1,2,0:T(8,128)} fusion(bf16[1,2048,4,1024]{1,3,2,0:T(8,128)(2,1)} %copy.59, bf16[128,8,2048,1]{2,0,1,3:T(8,128)(2,1)} %bitcast.96), kind=kOutput, calls=%fused_computation.4 | convolution fusion | flops 17179869184 | bytes 37748736 | tf_op jit(solution)/shard_map/dot_general | solution.py:37
  226.6 20.7 %fusion.15 = bf16[128,4,8,1024]{3,2,1,0:T(8,128)(2,1)} fusion(f32[8,8,4,4,1]{1,0,3,2,4:T(8,128)S(1)} %bitcast.95, f32[128,8,4,1024]{3,1,2,0:T(8,128)} %fusion.4), kind=kOutput, calls=%fused_computation.14 | convolution fusion | flops 1614807040 | bytes 25169920 | tf_op jit(solution)/shard_map/kypq,akqb->apyb/dot_general | solution.py:43
  247.3 123.3 %all-gather.8.cloned.1.call-done = bf16[2048,8,1024]{2,0,1:T(8,128)(2,1)} async-done(((bf16[128,8,1024]{2,0,1:T(8,128)(2,1)}), bf16[2048,8,1024]{2,0,1:T(8,128)(2,1)}) %all-gather.8.cloned.1.call-update) | async-done | bytes 33554448 | tf_op jit(solution)/shard_map/all_gather | solution.py:47
  370.6 46.6 %fusion.19 = f32[128,4,2048]{2,0,1:T(8,128)} fusion(bf16[2048,8,1024]{2,0,1:T(8,128)(2,1)} %all-gather.8.cloned.1.call-done, bf16[128,4,8,1024]{3,2,1,0:T(8,128)(2,1)} %fusion.15), kind=kOutput, calls=%fused_computation.16 | convolution fusion | flops 17179869184 | bytes 46137344 | tf_op jit(solution)/shard_map/dot_general | solution.py:49
  417.9 54.5 %fusion.29 = f32[8,8]{1,0:T(8,128)S(1)} fusion(f32[8,128,4,1024]{3,2,1,0:T(4,128)} %param.12), kind=kOutput, calls=%fused_computation.28 | convolution fusion | flops 402653184 | bytes 16777472 | tf_op jit(solution)/shard_map/japb,kapb->jk/dot_general | solution.py:58
  472.5 68.0 %all-gather.1 = f32[256,8]{1,0:T(8,128)S(1)} all-gather(f32[8,8]{1,0:T(8,128)S(1)} %fusion.29), channel_id=3, replica_groups=mesh['blk'=16,'cuts'=2] {'blk','cuts'}, dimensions={0}, use_global_device_ids=true | all-gather | bytes 8448 | tf_op jit(solution)/shard_map/all_gather | solution.py:59
  540.5 0.6 fusion.44
  541.2 43.3 %fusion.32 = f32[8]{0:T(128)S(1)} fusion(f32[8,128,4,1024]{3,2,1,0:T(4,128)} %param.12, f32[128,4,1024,1]{2,0,1,3:T(8,128)} %bitcast.92), kind=kOutput, calls=%fused_computation.29 | convolution fusion | flops 50331648 | bytes 18874400 | tf_op jit(solution)/shard_map/japb,apb->j/dot_general | solution.py:60
  584.5 1.1 multiply_reduce_fusion
  586.3 37.1 %all-reduce = (f32[8]{0:T(128)S(1)}, f32[]{:T(128)}) all-reduce(f32[8]{0:T(128)S(1)} %fusion.32, f32[]{:T(128)} %multiply_reduce_fusion), channel_id=1, replica_groups=mesh['blk'=16,'cuts'=2] {'blk','cuts'}, use_global_device_ids=true, to_apply=%region_1.0 | all-reduce | flops 9 | bytes 72 | tf_op jit(solution)/shard_map/psum | solution.py:61
  623.4 0.6 fusion.45
  624.0 0.9 multiply_reduce_fusion.3
  627.4 0.7 multiply_reduce_fusion.4
  628.1 30.9 %fusion.6 = f32[1,128,4,1024]{3,0,2,1:T(1,128)} fusion(f32[8,128,4,1024]{3,2,1,0:T(4,128)} %param.12, f32[8]{0:T(128)S(1)} %get-tuple-element.23), kind=kOutput, calls=%fused_computation.7 | convolution fusion | flops 50331648 | bytes 18874400 | tf_op jit(solution)/shard_map/j,japb->apb/dot_general | solution.py:86
  659.0 0.7 multiply_reduce_fusion.1
  663.5 6.9 %fusion.27 = f32[128,4,1024]{2,0,1:T(8,128)S(1)} fusion(f32[1,128,4,1024]{3,2,1,0:T(4,128)} %get-tuple-element.25, f32[128,4,1024]{2,0,1:T(8,128)S(1)} %copy-done.2, f32[1,128,4,1024]{3,0,2,1:T(1,128)} %fusion.6, f32[1,128,4,1024]{3,2,1,0:T(4,128)} %copy-done.3, f32[]{:T(128)} %sqrt.3, f32[]{:T(128)S(6)} %copy.129, f32[]{:T(128)} %bitcast.27), kind=kLoop, calls=%fused_computation.21 | loop fusion | flops 3145728 | bytes 10485772 | tf_op jit(solution)/shard_map/div | solution.py:90
  670.4 2.7 copy.71
  (26 shorter events, 0.2 us)
Async XLA Ops:
  7.2 49.4 %copy-start = (f32[8,8,2,2]{1,3,2,0:T(2,128)S(1)}, f32[8,8,2,2]{1,3,2,0:T(2,128)}, u32[]{:S(2)}) copy-start(f32[8,8,2,2]{1,3,2,0:T(2,128)} %param.10) | copy-start | bytes 3076
  7.2 137.3 %all-gather.10.cloned.1.call-start = ((), (), s32[]{:S(2)}) async-start(), calls=%async_computation.5 | async-start | bytes 17825792 | tf_op jit(solution)/shard_map/all_gather | solution.py:35
  11.7 1.3 copy-start.3
  11.7 3.5 copy-start.4
  15.2 185.8 %all-gather.6.cloned.1.call-start = ((), (), s32[]{:S(2)}) async-start(), calls=%async_computation.2 | async-start | bytes 6291456 | tf_op jit(solution)/shard_map/all_gather | solution.py:28
  17.8 352.9 %all-gather.8.cloned.1.call-start = ((), (), s32[]{:S(2)}) async-start(), calls=%async_computation.3 | async-start | bytes 35651584 | tf_op jit(solution)/shard_map/all_gather | solution.py:47
  53.6 2.8 copy-start.6
  53.6 2.8 copy-start.7
  56.3 484.9 %reduce-scatter.2.cloned.1.call-start = ((), (), s32[]{:S(2)}) async-start(), calls=%async_computation.4 | async-start | bytes 6291456 | tf_op jit(solution)/shard_map/reduce_scatter | solution.py:52
  201.0 25.6 %copy-start.5 = (f32[8,8,2,2,2,2]{1,0,5,4,3,2:T(8,128)S(1)}, f32[8,8,2,2,2,2]{1,0,5,4,3,2:T(8,128)}, u32[]{:S(2)}) copy-start(f32[8,8,2,2,2,2]{1,0,5,4,3,2:T(8,128)} %copy.63) | copy-start | bytes 12292
  541.2 43.3 %copy-start.2 = (f32[128,4,1024]{2,0,1:T(8,128)S(1)}, f32[128,4,1024]{2,0,1:T(8,128)}, u32[]{:S(2)}) copy-start(f32[128,4,1024]{2,0,1:T(8,128)} %reduce-scatter.2.cloned.1.call-done) | copy-start | bytes 6291460
  663.4 9.6 %copy-start.1 = (f32[8,8,2,2]{1,3,2,0:T(2,128)S(1)}, f32[8,8,2,2]{1,3,2,0:T(2,128)}, u32[]{:S(2)}) copy-start(f32[8,8,2,2]{1,3,2,0:T(2,128)} %param.10) | copy-start | bytes 3076
Sparse Core Ops, SparseCore 0:
  15.3 129.1 all-gather.9
  146.1 54.8 all-gather.5
  202.5 168.0 all-gather.7
  417.4 54.3 reduce-scatter.1
